TPU v7x, 32 devices: a 4x4x1 block of a 4x4x8 slice. The times are simulated.
32 devices in a mesh: dp: 1 (over z), col: 4 (over y), row: 8 (over x, core).
Axes of the slice: x: 4, y: 4, z: 1, core: 2. Of those that a mesh axis runs over, the one named last changes fastest.
The devices are a block of a 4x4x8 slice.
Arguments:
- hidden: bfloat16 [64, 4096], P('dp', 'row')
- cache_len: int32 [64], P('dp')
- k_cache: bfloat16 [2, 64, 32, 256, 128], P(None, 'dp', ('col', 'row'))
- v_cache: bfloat16 [2, 64, 32, 256, 128], P(None, 'dp', ('col', 'row'))
- ln1_g: bfloat16 [2, 4096], P(None, 'row')
- ln1_b: bfloat16 [2, 4096], P(None, 'row')
- w_q: bfloat16 [2, 4096, 4096], P(None, 'row', 'col')
- b_q: bfloat16 [2, 4096], P(None, 'col')
- w_k: bfloat16 [2, 4096, 4096], P(None, 'row', 'col')
- b_k: bfloat16 [2, 4096], P(None, 'col')
- w_v: bfloat16 [2, 4096, 4096], P(None, 'row', 'col')
- b_v: bfloat16 [2, 4096], P(None, 'col')
- w_o: bfloat16 [2, 4096, 4096], P(None, 'col', 'row')
- b_o: bfloat16 [2, 4096], P(None, 'row')
- ln2_g: bfloat16 [2, 4096], P(None, 'row')
- ln2_b: bfloat16 [2, 4096], P(None, 'row')
- w_fc1: bfloat16 [2, 4096, 16384], P(None, 'row', 'col')
- b_fc1: bfloat16 [2, 16384], P(None, 'col')
- w_fc2: bfloat16 [2, 16384, 4096], P(None, 'col', 'row')
- b_fc2: bfloat16 [2, 4096], P(None, 'row')
Outputs:
- output 1: bfloat16 [64, 4096], P('dp', 'row')
- output 2: bfloat16 [2, 64, 32, 128], P(None, 'dp', ('col', 'row'))
- output 3: bfloat16 [2, 64, 32, 128], P(None, 'dp', ('col', 'row'))
All inputs are finite; a program needn't handle non-finite values.
Results may differ from a plain program's by a relative error of at most 0.02.
Values are sent between devices in bfloat16 or wider.
A program may use at most 768 MiB of HBM per device.

v0:
```python
import functools

import jax
import jax.numpy as jnp
from jax import lax
from jax.experimental import pallas as pl
from jax.experimental.pallas import tpu as pltpu
from jax.sharding import PartitionSpec as P

EPS_LN = 1e-5
VLIM = 64 * 1000 * 1000
MESH = pl.DeviceIdType.MESH
F32 = jnp.float32
BF16 = jnp.bfloat16


class Sems:
    def __init__(self):
        self.count = 0

    def take(self, n):
        base = self.count
        self.count += n
        return base


HALVES = 2


def layout():
    recv = dict(st1=1, st1p=1, st2=1, st2p=1, q=1, vd=1, k=1, v=1, ag=1, wo=1, fd=2, fi=1, fg=1, ug=5, fo=1)
    send = dict(st1=1, st2=1, q=1, vd=1, k=1, v=1, ag=1, wo=1, fd=1, fi=1, fg=1, ug=1, fo=1)
    tables = []
    for names in (send, recv):
        sems = Sems()
        tables.append(([{name: sems.take(n) for name, n in names.items()} for _ in range(HALVES)], sems))
    return [t for t, _ in tables], [c.count for _, c in tables]


SENT_WITH = dict(st1p="st1", st2p="st2")


def kernel(dims, hid_hbm, len_hbm, kc_hbm, vc_hbm, g1_hbm, b1_hbm, wq_hbm, bq_hbm, wk_hbm, bk_hbm, wv_hbm, bv_hbm,
           wo_hbm, bo_hbm, g2_hbm, b2_hbm, w1_hbm, bf1_hbm, w2_hbm, bf2_hbm,
           h_out, k_out, v_out, local, halves, state, kt, sem):
    n_layer, n_row, n_col, table = dims
    hid_v, len_v, kc, vc, g1, b1, wq, bq, wk, bk, wv, bv, wo, bo, g2, b2, w1, bf1, w2, bf2 = local
    small_sem, big_sem, ssem, rsem = sem
    n_chip = n_row // 2
    row = lax.axis_index("row")
    col = lax.axis_index("col")
    chip = row // 2
    par = row % 2
    partner = row + 1 - 2 * par
    batch, width = hid_v.shape
    part = batch // HALVES
    hd = kc.shape[-1]
    keys = kc.shape[2]
    ffb = w1.shape[-1] // n_row
    lanes = ffb // 128
    offs = [2, 1, 3, 0]
    chips = {off: lax.rem(chip + off, n_chip) for off in offs}
    row_order = []
    for off in offs[:-1]:
        row_order += [2 * chips[off] + par, 2 * chips[off] + 1 - par]

    barrier = pltpu.get_barrier_semaphore()
    for t in range(1, n_row):
        pl.semaphore_signal(barrier, inc=1, device_id={"row": lax.rem(row + t, n_row)}, device_id_type=MESH)
    for t in range(1, n_col):
        pl.semaphore_signal(barrier, inc=1, device_id={"col": lax.rem(col + t, n_col)}, device_id_type=MESH)

    small = [(hid_hbm, hid_v), (g1_hbm, g1), (b1_hbm, b1), (len_hbm, len_v), (bq_hbm, bq), (bk_hbm, bk),
             (bv_hbm, bv), (bo_hbm, bo), (g2_hbm, g2), (b2_hbm, b2), (bf1_hbm, bf1), (bf2_hbm, bf2)]
    small_copies = [pltpu.make_async_copy(s, d, small_sem.at[i]) for i, (s, d) in enumerate(small)]
    bigs = [(wq_hbm, wq), (wk_hbm, wk), (wv_hbm, wv), (kc_hbm, kc), (vc_hbm, vc), (wo_hbm, wo), (w1_hbm, w1),
            (w2_hbm, w2)]
    WQ, WK, WV, KC, VC, WO, W1, W2 = range(8)

    def big_copy(i, l):
        s, d = bigs[i]
        src = s.at[l, :, 0] if i in (KC, VC) else s.at[l]
        return pltpu.make_async_copy(src, d.at[l], big_sem.at[l, i])

    for c in small_copies[:3]:
        c.start()
    for i in (WQ, WK, WV):
        big_copy(i, 0).start()
    for c in small_copies[3:]:
        c.start()
    small_copies[0].wait()
    state[...] = hid_v[...]


    def enter():
        pl.semaphore_wait(barrier, n_row - 1 + n_col - 1)

    def norm_vectors():
        for c in small_copies[1:3]:
            c.wait()

    def rest_of_loads():
        for c in small_copies[3:]:
            c.wait()
        for i in (KC, VC, WO, W1, W2):
            big_copy(i, 0).start()
        for l in range(1, n_layer):
            for i in range(8):
                big_copy(i, l).start()

    def remote(h, name, i, src, dst, axis, target):
        return pltpu.make_async_remote_copy(
            src_ref=src, dst_ref=dst, send_sem=ssem.at[table[0][h][SENT_WITH.get(name, name)]],
            recv_sem=rsem.at[table[1][h][name] + i], device_id={axis: target}, device_id_type=MESH)

    def same_bytes(h, name, i, ref, axis):
        return remote(h, name, i, ref, ref, axis, partner if axis == "row" else lax.rem(col + 1, n_col))

    def got(h, name, i, ref, axis="row"):
        same_bytes(h, name, i, ref, axis).wait_recv()

    def sent(h, name, ref, axis="row"):
        same_bytes(h, name, 0, ref, axis).wait_send()

    def pick(ref, l):
        rows = ref[...].astype(F32)
        out = rows[0:1]
        for i in range(1, n_layer):
            out = jnp.where(l == i, rows[i:i + 1], out)
        return out

    def pick_slice(ref, l, start, size):
        rows = ref[:, pl.ds(pl.multiple_of(start, size), size)].astype(F32)
        out = rows[0:1]
        for i in range(1, n_layer):
            out = jnp.where(l == i, rows[i:i + 1], out)
        return out

    eye = lax.broadcasted_iota(jnp.int32, (part, 128), 0) == lax.broadcasted_iota(jnp.int32, (part, 128), 1)

    def to_row(column):
        return jnp.sum(jnp.where(eye, column, 0.0), axis=0, keepdims=True)

    def to_column(line):
        return jnp.sum(jnp.where(eye, line, 0.0), axis=1, keepdims=True)

    def local_norm(l, h, name, which, gain, shift, entering=False):
        st_send, st_recv = halves[h]["st_send"], halves[h]["st_recv"]
        x = state[h * part:(h + 1) * part].astype(F32)
        c = jnp.sum(x, axis=1, keepdims=True) / width
        xc = x - c
        v = jnp.sum(xc * xc, axis=1, keepdims=True) / width
        sub = lax.broadcasted_iota(jnp.int32, (8, 128), 0)
        tile = jnp.where(sub == 0, to_row(c), jnp.where(sub == 1, to_row(v), 0.0))
        st_send[l, which] = tile
        st_recv[l, which, row] = tile

        def send():
            for j in row_order:
                remote(h, name, 0, st_send.at[l, which], st_recv.at[l, which, row], "row", j).start()
            remote(h, name + "p", 0, st_send.at[l, which], st_recv.at[l, which, row], "row", partner).start()

        if entering:
            norm_vectors()
        else:
            send()
        g, b = pick(gain, l), pick(shift, l)
        y = (xc * lax.rsqrt(v + EPS_LN) * g).astype(BF16)
        if h:
            return y, send
        extra = lax.broadcasted_iota(jnp.int32, (16, 1), 0)
        extra = jnp.where(extra == 0, g, jnp.where(extra == 1, b, 0.0))
        return jnp.concatenate([y, extra.astype(BF16)], axis=0), send

    def scale_of(v):
        return (v + EPS_LN) * lax.rsqrt(v + EPS_LN)

    def global_norm(parts):
        m = sum(c for c, _ in parts) / len(parts)
        var = sum(v + (c - m) * (c - m) for c, v in parts) / len(parts)
        r = lax.rsqrt(var + EPS_LN)
        return [(to_column(r * scale_of(v)), to_column(r * (c - m))) for c, v in parts]

    def stats(l, h, which, j):
        tile = halves[h]["st_recv"][l, which, j]
        return tile[0:1], tile[1:2]

    def merge(one, two):
        half = 0.5 * (one[0] - two[0])
        return 0.5 * (one[0] + two[0]), 0.5 * (one[1] + two[1]) + half * half

    def pair_merge(l, h, which):
        here, there = stats(l, h, which, row), stats(l, h, which, partner)
        c_pair, v_pair = merge(here, there)
        r_pair = lax.rsqrt(v_pair + EPS_LN)
        a_own, a_got = to_column(r_pair * scale_of(here[1])), to_column(r_pair * scale_of(there[1]))
        d_own = to_column(r_pair * (here[0] - c_pair))

        def rows(own, other, g_own, g_other):
            return (a_own * own[:part] + a_got * other[:part]) + d_own * (g_own - g_other)

        return rows

    def pair_coefficients(l, h, which):
        return global_norm([merge(stats(l, h, which, 2 * k), stats(l, h, which, 2 * k + 1)) for k in range(n_chip)])

    def col_send(l, h, name, value):
        buf = halves[h][name]
        buf[l, col] = value.astype(BF16)
        for t in (2, 1, 3):
            remote(h, name, 0, buf.at[l, col], buf.at[l, col], "col", lax.rem(col + t, n_col)).start()

    def col_sum(l, h, name, bias):
        buf = halves[h][name]
        got(h, name, 0, buf.at[l, pl.ds(0, n_col - 1)], "col")
        total = buf[l, 0].astype(F32)
        for j in range(1, n_col):
            total = total + buf[l, j].astype(F32)
        rows = slice(h * part, (h + 1) * part)
        state[rows] = (state[rows].astype(F32) + (total + bias)).astype(BF16)
        sent(h, name, buf.at[l, pl.ds(0, n_col - 1)], "col")

    def product(l, h, w, weight):
        b = halves[h]
        res = jnp.dot(b["y"][...], weight[l], preferred_element_type=F32).astype(BF16)
        for j in range(n_row):
            b["q_send"][l, w, j] = res[:, j * hd:(j + 1) * hd]

    def send_product(l, h, w):
        b = halves[h]
        for j in row_order + [partner]:
            remote(h, ("q", "k")[w], 0, b["q_send"].at[l, w, j], b["q_recv"].at[l, w, row], "row", j).start()
        b["q_recv"][l, w, row] = b["q_send"][l, w, row]

    def project_q(l, h, entering=False):
        y, send_stats = local_norm(l, h, "st1", 0, g1, b1, entering)
        halves[h]["y"][...] = y
        if h:
            project_v(l, h)
        if h == 0:
            big_copy(WQ, l).wait()
        product(l, h, 0, wq)
        if entering:
            enter()
            send_stats()

    def project_kv(l, h):
        b = halves[h]
        if h == 0:
            big_copy(WK, l).wait()
        product(l, h, 1, wk)
        send_product(l, h, 1)
        if h == 0:
            project_v(l, h)

    def project_v(l, h):
        b = halves[h]
        if h == 0:
            big_copy(WV, l).wait()
        res = jnp.dot(b["y"][...], wv[l], preferred_element_type=F32)
        even = jnp.concatenate([res[:, 2 * k * hd:(2 * k + 1) * hd] for k in range(n_chip)], axis=1)
        odd = jnp.concatenate([res[:, (2 * k + 1) * hd:(2 * k + 2) * hd] for k in range(n_chip)], axis=1)
        b["vd_send"][l] = jnp.where(par == 0, odd, even).astype(BF16)
        remote(h, "vd", 0, b["vd_send"].at[l], b["vd_recv"].at[l], "row", partner).start()
        b["v_mine"][...] = jnp.where(par == 0, even, odd)

    def send_v(l, h):
        b, first = halves[h], halves[0]
        got(h, "st1p", 0, b["st_recv"].at[l, 0, 0])
        merged = pair_merge(l, h, 0)
        got(h, "vd", 0, b["vd_recv"].at[l])
        own, other = b["v_mine"][...], b["vd_recv"][l].astype(F32)
        gb_own, gb_other = first["v_mine"][part:], first["vd_recv"][l, part:].astype(F32)
        both = merged(own, other, gb_own[0:1], gb_other[0:1])
        if h == 0:
            both = jnp.concatenate([both, gb_own + gb_other], axis=0)
        both = both.astype(BF16)
        for k in range(n_chip):
            b["v_send"][l, k] = both[:, k * hd:(k + 1) * hd]
        for off in offs[:-1]:
            k = chips[off]
            remote(h, "v", 0, b["v_send"].at[l, k], b["v_recv"].at[l, chip], "row", 2 * k + par).start()
        b["v_recv"][l, chip] = b["v_send"][l, chip]

    def collect(parts, firsts, coefs, bias, l):
        total = pick_slice(bias, l, row * hd, hd)
        for value, first, (scale, shift) in zip(parts, firsts, coefs):
            gb = first.astype(F32)
            total = total + (scale * value[:part].astype(F32) + (shift * gb[0:1] + gb[1:2]))
        return total

    def ready_q(l, h):
        b, first = halves[h], halves[0]
        got(h, "st1", 0, b["st_recv"].at[l, 0, pl.ds(0, n_row - 2)])
        coef = global_norm([stats(l, h, 0, j) for j in range(n_row)])
        coef_pair = pair_coefficients(l, h, 0)
        got(h, "q", 0, b["q_recv"].at[l, 0, pl.ds(0, n_row - 1)])
        q = collect([b["q_recv"][l, 0, j] for j in range(n_row)],
                    [first["q_recv"][l, 0, j, part:] for j in range(n_row)], coef, bq, l)
        b["q"][...] = (q * (hd ** -0.5)).astype(BF16).astype(F32)
        return coef, coef_pair

    def attend(l, h, coefs):
        coef, coef_pair = coefs
        b, first = halves[h], halves[0]
        base = h * part
        q = b["q"][...]
        group = 16
        rowi = lax.broadcasted_iota(jnp.int32, (group, 1), 0)
        parts = []
        for g in range(part // group):
            q_g = q[g * group:(g + 1) * group]
            lhs = jnp.concatenate([jnp.where(rowi == i, q_g, 0.0) for i in range(group)], axis=1).astype(BF16)
            k_g = jnp.concatenate([kt[base + g * group + i] for i in range(group)], axis=0)
            parts.append(jnp.dot(lhs, k_g, preferred_element_type=F32))
        scores = jnp.concatenate(parts, axis=0)
        spread = lax.broadcasted_iota(jnp.int32, (part, batch), 0) + base
        spread = spread == lax.broadcasted_iota(jnp.int32, (part, batch), 1)
        lens = jnp.sum(jnp.where(spread, len_v[...], 0), axis=1, keepdims=True)
        scores = jnp.where(lax.broadcasted_iota(jnp.int32, (part, keys), 1) < lens, scores, -jnp.inf)

        got(h, "k", 0, b["q_recv"].at[l, 1, pl.ds(0, n_row - 1)])
        k_new = collect([b["q_recv"][l, 1, j] for j in range(n_row)],
                        [first["q_recv"][l, 1, j, part:] for j in range(n_row)], coef, bk, l).astype(BF16)
        s_new = jnp.sum(q * k_new.astype(F32), axis=1, keepdims=True)
        peak = jnp.maximum(jnp.max(scores, axis=1, keepdims=True), s_new)
        e = jnp.exp(scores - peak)
        e_new = jnp.exp(s_new - peak)
        mass = jnp.sum(e, axis=1, keepdims=True) + e_new
        prob = (e / mass).astype(BF16).astype(F32)
        prob_new = (e_new / mass).astype(BF16).astype(F32)
        if h == 0:
            big_copy(VC, l).wait()
        outs = []
        for g in range(part // group):
            p_g = prob[g * group:(g + 1) * group]
            lhs = jnp.concatenate([jnp.where(rowi // 2 == i, p_g, 0.0) for i in range(group // 2)],
                                  axis=1).astype(BF16)
            at = base + g * group
            v_g = jnp.concatenate([jnp.concatenate([vc[l, at + 2 * i], vc[l, at + 2 * i + 1]], axis=1)
                                   for i in range(group // 2)], axis=0)
            out = jnp.dot(lhs, v_g, preferred_element_type=F32)
            outs.append(jnp.where(rowi % 2 == 0, out[:, :hd], out[:, hd:]))
        got(h, "v", 0, b["v_recv"].at[l, pl.ds(0, n_chip - 1)])
        v_new = collect([b["v_recv"][l, k] for k in range(n_chip)],
                        [first["v_recv"][l, k, part:] for k in range(n_chip)], coef_pair, bv, l).astype(BF16)
        mixed = jnp.concatenate(outs, axis=0) + prob_new * v_new.astype(F32)
        b["ag"][l, row] = mixed.astype(BF16)
        for j in row_order + [partner]:
            remote(h, "ag", 0, b["ag"].at[l, row], b["ag"].at[l, row], "row", j).start()
        k_out[l, base:base + part] = k_new
        v_out[l, base:base + part] = v_new

    def out_product(l, h):
        ag = halves[h]["ag"]
        if h == 0:
            big_copy(WO, l).wait()
        got(h, "ag", 0, ag.at[l, pl.ds(0, n_row - 1)])
        gathered = jnp.concatenate([ag[l, j] for j in range(n_row)], axis=1)
        col_send(l, h, "wo", jnp.dot(gathered, wo[l], preferred_element_type=F32))

    def up(l, h):
        b, first = halves[h], halves[0]
        col_sum(l, h, "wo", pick(bo, l))
        y2, _ = local_norm(l, h, "st2", 1, g2, b2)
        if h == 0:
            big_copy(W1, l).wait()

        def block(j):
            return jnp.dot(y2, w1[l, :, pl.ds(pl.multiple_of(j * ffb, ffb), ffb)], preferred_element_type=F32)

        for some in (offs[:2], offs[2:]):
            blocks = [block(2 * chips[off] + 1 - par).astype(BF16) for off in some]
            for off, value in zip(some, blocks):
                b["fd_send"][l, chips[off]] = value
            for off in some:
                k = chips[off]
                remote(h, "fd", offs.index(off) // 2, b["fd_send"].at[l, k], b["fd_recv"].at[l, k], "row",
                       partner).start()
        blocks = [block(2 * chips[off] + par) for off in offs[:-1]]
        for off, value in zip(offs, blocks):
            b["f_mine"][chips[off]] = value
        got(h, "st2p", 0, b["st_recv"].at[l, 1, 0])
        merged = pair_merge(l, h, 1)
        for off in offs:
            k = chips[off]
            if off == 0:
                b["f_mine"][k] = block(2 * k + par)
            if off in (offs[0], offs[2]):
                got(h, "fd", offs.index(off) // 2, b["fd_recv"].at[l, pl.ds(0, 2)])
            gb_own, gb_other = first["f_mine"][k, part:], first["fd_recv"][l, k, part:].astype(F32)
            both = merged(b["f_mine"][k], b["fd_recv"][l, k].astype(F32), gb_own[0:1], gb_other[0:1]).astype(BF16)
            if h == 0:
                gb = gb_own + gb_other
                gb = jnp.concatenate([gb[0:1], gb[1:2]], axis=1)
                tile = jnp.concatenate([gb[:, i * 128:(i + 1) * 128] for i in range(2 * lanes)], axis=0)
            if off:
                b["fi_send"][l, k] = both
                remote(h, "fi", 0, b["fi_send"].at[l, k], b["fi_recv"].at[l, chip], "row", 2 * k + par).start()
                if h == 0:
                    b["fg_send"][l, k] = tile
                    remote(h, "fg", 0, b["fg_send"].at[l, k], b["fg_recv"].at[l, chip], "row", 2 * k + par).start()
            else:
                b["fi_recv"][l, k] = both
                if h == 0:
                    b["fg_recv"][l, k] = tile

    def activate(l, h):
        b, first = halves[h], halves[0]
        ug = b["ug"]
        got(h, "st2", 0, b["st_recv"].at[l, 1, pl.ds(0, n_row - 2)])
        coef = pair_coefficients(l, h, 1)
        total = pick_slice(bf1, l, row * ffb, ffb)
        if h == 0:
            got(h, "fg", 0, b["fg_recv"].at[l, pl.ds(0, n_chip - 1)])
        got(h, "fi", 0, b["fi_recv"].at[l, pl.ds(0, n_chip - 1)])
        for k in range(n_chip):
            tile = first["fg_recv"][l, k]
            g = jnp.concatenate([tile[i:i + 1] for i in range(lanes)], axis=1)
            shift = jnp.concatenate([tile[lanes + i:lanes + i + 1] for i in range(lanes)], axis=1)
            total = total + (coef[k][0] * b["fi_recv"][l, k].astype(F32) + (coef[k][1] * g + shift))
        ug[l, row] = jnp.maximum(total.astype(BF16), 0)
        for off in offs[:-1]:
            remote(h, "ug", 2 - off % 2, ug.at[l, row], ug.at[l, row], "row", 2 * chips[off] + par).start()
        remote(h, "ug", 0, ug.at[l, row], ug.at[l, row], "row", partner).start()

    def same(off):
        return 2 * chips[off] + par

    def cross(off):
        return 2 * chips[off] + 1 - par

    def fc2_block(l, h, j):
        return jnp.dot(halves[h]["ug"][l, j], w2[l, pl.ds(pl.multiple_of(j * ffb, ffb), ffb), :],
                       preferred_element_type=F32)

    def pass_on(l, h, off):
        ug = halves[h]["ug"]
        remote(h, "ug", 4 - off % 2, ug.at[l, same(off)], ug.at[l, same(off)], "row", partner).start()

    def down_first(l, h):
        if h == 0:
            big_copy(W2, l).wait()
        got(h, "ug", 0, halves[h]["ug"].at[l, partner])
        halves[h]["acc"][...] = fc2_block(l, h, row) + fc2_block(l, h, partner)

    def down_near(l, h):
        got(h, "ug", 1, halves[h]["ug"].at[l, pl.ds(0, 2)])
        pass_on(l, h, 1)
        pass_on(l, h, 3)
        acc = halves[h]["acc"]
        acc[...] = acc[...] + (fc2_block(l, h, same(1)) + fc2_block(l, h, same(3)))

    def down_far(l, h):
        ug, acc = halves[h]["ug"], halves[h]["acc"]
        got(h, "ug", 2, ug.at[l, same(2)])
        pass_on(l, h, 2)
        got(h, "ug", 3, ug.at[l, pl.ds(0, 2)])
        acc[...] = acc[...] + (fc2_block(l, h, same(2)) + fc2_block(l, h, cross(1)) + fc2_block(l, h, cross(3)))

    def down_last(l, h):
        got(h, "ug", 4, halves[h]["ug"].at[l, cross(2)])
        col_send(l, h, "fo", halves[h]["acc"][...] + fc2_block(l, h, cross(2)))

    def drain(l, h):
        b = halves[h]
        for which, name in ((0, "st1"), (1, "st2")):
            sent(h, name, b["st_recv"].at[l, which, pl.ds(0, n_row - 1)])
        sent(h, "q", b["q_recv"].at[l, 0, pl.ds(0, n_row - 1)])
        sent(h, "k", b["q_recv"].at[l, 1, pl.ds(0, n_row - 1)])
        sent(h, "vd", b["vd_send"].at[l])
        sent(h, "v", b["v_send"].at[l, pl.ds(0, n_chip - 1)])
        sent(h, "ag", b["ag"].at[l, pl.ds(0, n_row - 1)])
        sent(h, "fd", b["fd_send"].at[l])
        sent(h, "fi", b["fi_send"].at[l, pl.ds(0, n_chip - 1)])
        if h == 0:
            sent(h, "fg", b["fg_send"].at[l, pl.ds(0, n_chip - 1)])
        sent(h, "ug", b["ug"].at[l, pl.ds(0, n_row - 1)])

    def turn_keys(l, h):
        step = 8

        def some(i, carry):
            for j in range(step):
                at = h * part + i * step + j
                kt[at] = kc[l, at].T
            return carry

        if h == 0:
            big_copy(KC, l).wait()
        lax.fori_loop(0, part // step, some, 0)

    def layer(l, carry):
        def later():
            finish_layer(l - 1, 0)
            project_q(l, 0)

        pl.when(l > 0)(later)
        send_product(l, 0, 0)
        project_kv(l, 0)
        pl.when(l == 0)(rest_of_loads)
        send_v(l, 0)
        for h in range(1, HALVES):
            pl.when(l > 0)(functools.partial(finish_layer, l - 1, h))
            project_q(l, h)
            send_product(l, h, 0)
            project_kv(l, h)
        pl.when(l == 0)(functools.partial(turn_keys, 0, 0))
        coefs = ready_q(l, 0)
        send_v(l, HALVES - 1)
        attend(l, 0, coefs)
        pl.when(l == 0)(functools.partial(turn_keys, 0, 1))
        for h in range(1, HALVES):
            attend(l, h, ready_q(l, h))
        for stage in (out_product, up, activate, down_first):
            for h in range(HALVES):
                stage(l, h)
        pl.when(l + 1 < n_layer)(lambda: turn_keys(l + 1, 0))
        for h in range(HALVES):
            down_near(l, h)
            down_far(l, h)
            down_last(l, h)
        for h in range(HALVES):
            drain(l, h)
        pl.when(l + 1 < n_layer)(lambda: turn_keys(l + 1, 1))
        return carry

    def finish_layer(l, h):
        col_sum(jnp.maximum(l, 0), h, "fo", pick(bf2, l))

    project_q(0, 0, entering=True)
    lax.fori_loop(0, n_layer, layer, 0)
    for h in range(HALVES):
        finish_layer(n_layer - 1, h)
    h_out[...] = state[...]


def finish(h, k, v, h_out, k_out, v_out, sem):
    copies = [pltpu.make_async_copy(s, d, sem.at[i]) for i, (s, d) in enumerate(((h, h_out), (k, k_out), (v, v_out)))]
    for c in copies:
        c.start()
    for c in copies:
        c.wait()


def solution(mesh):
    n_row, n_col = mesh.shape["row"], mesh.shape["col"]
    n_chip = n_row // 2
    act_spec = P("dp", "row")
    cache_spec = P(None, "dp", ("col", "row"), None, None)
    fresh_spec = P(None, "dp", ("col", "row"), None)
    in_weight = P(None, "row", "col")
    out_weight = P(None, "col", "row")
    col_vec = P(None, "col")
    row_vec = P(None, "row")
    in_specs = (act_spec, P("dp"), cache_spec, cache_spec, row_vec, row_vec,
                in_weight, col_vec, in_weight, col_vec, in_weight, col_vec,
                out_weight, row_vec, row_vec, row_vec, in_weight, col_vec, out_weight, row_vec)

    def local_step(hidden, cache_len, k_cache, v_cache, ln1_g, ln1_b, w_q, b_q, w_k, b_k, w_v, b_v,
                   w_o, b_o, ln2_g, ln2_b, w_fc1, b_fc1, w_fc2, b_fc2):
        batch, width = hidden.shape
        n_layer, _, _, keys, hd = k_cache.shape
        ff = w_fc1.shape[2]
        ffb = ff // n_row
        table, n_sem = layout()
        part = batch // HALVES
        args = (hidden, cache_len.reshape(1, batch), k_cache, v_cache, ln1_g, ln1_b, w_q, b_q, w_k, b_k, w_v, b_v,
                w_o, b_o, ln2_g, ln2_b, w_fc1, b_fc1, w_fc2, b_fc2)

        def vm(shape, dtype=BF16):
            return pltpu.VMEM(shape, dtype)

        local = [vm(a.shape, a.dtype) for a in args]
        local[2] = local[3] = vm((n_layer, batch, keys, hd))

        def half(h):
            rows = part + 16 if h == 0 else part
            gb = (n_layer, n_chip, 2 * ffb // 128, 128)
            shapes = dict(
                q_send=vm((n_layer, 2, n_row, rows, hd)), q_recv=vm((n_layer, 2, n_row, rows, hd)),
                vd_send=vm((n_layer, rows, n_chip * hd)), vd_recv=vm((n_layer, rows, n_chip * hd)),
                v_mine=vm((rows, n_chip * hd), F32),
                v_send=vm((n_layer, n_chip, rows, hd)), v_recv=vm((n_layer, n_chip, rows, hd)),
                y=vm((rows, width)), q=vm((part, hd), F32), ag=vm((n_layer, n_row, part, hd)),
                st_send=vm((n_layer, 2, 8, 128), F32), st_recv=vm((n_layer, 2, n_row, 8, 128), F32),
                wo=vm((n_layer, n_col, part, width)), fo=vm((n_layer, n_col, part, width)),
                fd_send=vm((n_layer, n_chip, rows, ffb)), fd_recv=vm((n_layer, n_chip, rows, ffb)),
                f_mine=vm((n_chip, rows, ffb), F32),
                fi_send=vm((n_layer, n_chip, part, ffb)), fi_recv=vm((n_layer, n_chip, part, ffb)),
                ug=vm((n_layer, n_row, part, ffb)), acc=vm((part, width), F32))
            if h == 0:
                shapes.update(fg_send=vm(gb, F32), fg_recv=vm(gb, F32))
            return shapes

        dma = pltpu.SemaphoreType.DMA
        scratch = [local, [half(h) for h in range(HALVES)], vm((batch, width)), vm((batch, hd, keys)),
                   [dma((12,)), dma((n_layer, 8)), dma((n_sem[0],)), dma((n_sem[1],))]]
        out_shape = (jax.ShapeDtypeStruct((batch, width), BF16),
                     jax.ShapeDtypeStruct((n_layer, batch, hd), BF16),
                     jax.ShapeDtypeStruct((n_layer, batch, hd), BF16))
        kept = pl.pallas_call(
            functools.partial(kernel, (n_layer, n_row, n_col, table)),
            out_shape=[pltpu.VMEM(o.shape, o.dtype) for o in out_shape],
            in_specs=[pl.BlockSpec(memory_space=pl.ANY)] * len(args),
            out_specs=[pl.BlockSpec(memory_space=pltpu.VMEM)] * 3,
            scratch_shapes=scratch,
            compiler_params=pltpu.CompilerParams(collective_id=0, has_side_effects=True, vmem_limit_bytes=VLIM),
        )(*args)
        h_out, k_new, v_new = pl.pallas_call(
            finish, out_shape=out_shape,
            in_specs=[pl.BlockSpec(memory_space=pltpu.VMEM)] * 3, out_specs=[pl.BlockSpec(memory_space=pl.ANY)] * 3,
            scratch_shapes=[pltpu.SemaphoreType.DMA((3,))],
        )(*[pltpu.with_memory_space_constraint(o, pltpu.VMEM) for o in kept])
        return h_out, k_new[:, :, None, :], v_new[:, :, None, :]

    return jax.shard_map(local_step, mesh=mesh, in_specs=in_specs,
                         out_specs=(act_spec, fresh_spec, fresh_spec), check_vma=False)
```

profile of v0, /device:TPU:97, one launch (start us, length us, event | category | flops | bytes accessed | tf_op | source)
XLA Modules:
  0.0 68.7 jit_solution(4657399620249461754)
XLA Ops:
  0.6 67.4 %shard_map.211 = (bf16[64,512]{1,0:T(8,128)(2,1)S(1)}, bf16[2,64,128]{2,1,0:T(8,128)(2,1)S(1)}, bf16[2,64,128]{2,1,0:T(8,128)(2,1)S(1)}) custom-call(bf16[64,512]{1,0:T(8,128)(2,1)} %hid_hbm.1, s32[1,64]{1,0:T(1,128)} %bitcast.7, bf16[2,64,1,256,128]{4,3,2,1,0:T(8,128)(2,1)} %kc_hbm.1, bf16[2,64,1,256,128]{4,3,2,1,0:T(8,128)(2,1)} %vc_hbm.1, ...), custom_call_target="tpu_custom_call" | custom-call | tf_op jit(solution)/shard_map/pallas_call | solution.py:602
  68.1 0.7 shard_map.212
where the time goes:
time: 68.8 us; the launch traced here: 68.7 us
  Pallas kernels  68.1 us (99%)
    pallas_call x1, Pallas kernels, local_step(): pl.pallas_call(functools.partial(kernel, (n_layer, n_row, n_col, table)),...  67.4 us

commit v1 on v0

--- a/solution.py
+++ b/solution.py
@@ -478,7 +478,7 @@
         sent(h, "ug", b["ug"].at[l, pl.ds(0, n_row - 1)])
 
     def turn_keys(l, h):
-        step = 8
+        step = 16
 
         def some(i, carry):
             for j in range(step):

time: 68.8 us -> 69.2 us (level)
  no operation moved by 1% of the time
where the time goes in v1:
time: 69.2 us; the launch traced here: 69.1 us
  Pallas kernels  68.5 us (99%)
    pallas_call x1, Pallas kernels, local_step(): pl.pallas_call(functools.partial(kernel, (n_layer, n_row, n_col, table)),...  67.8 us

profile of v1, /device:TPU:97, one launch (start us, length us, event | category | flops | bytes accessed | tf_op | source)
XLA Modules:
  0.0 69.1 jit_solution(2980311489949843087)
XLA Ops:
  0.6 67.8 %shard_map.211 = (bf16[64,512]{1,0:T(8,128)(2,1)S(1)}, bf16[2,64,128]{2,1,0:T(8,128)(2,1)S(1)}, bf16[2,64,128]{2,1,0:T(8,128)(2,1)S(1)}) custom-call(bf16[64,512]{1,0:T(8,128)(2,1)} %hid_hbm.1, s32[1,64]{1,0:T(1,128)} %bitcast.7, bf16[2,64,1,256,128]{4,3,2,1,0:T(8,128)(2,1)} %kc_hbm.1, bf16[2,64,1,256,128]{4,3,2,1,0:T(8,128)(2,1)} %vc_hbm.1, ...), custom_call_target="tpu_custom_call" | custom-call | tf_op jit(solution)/shard_map/pallas_call | solution.py:602
  68.5 0.7 shard_map.212
